TPU v7x, 32 devices: a whole 2x2x4 slice. The times are simulated.
32 devices in a mesh: groups: 2 (over y), gx: 8 (over z, x), gy: 2 (over core).
Axes of the slice: x: 2, y: 2, z: 4, core: 2. Of those that a mesh axis runs over, the one named last changes fastest.
Arguments:
- forcing: float32 [2, 512, 3072], P(None, ('groups', 'gx'), 'gy'), parts along dimension 1, may hold values from -6 to 6
- viscosity: float32 [512, 3072], P(('groups', 'gx'), 'gy'), parts along dimension 0, may hold values from 0.25 to 8
- mass: float32 [512, 3072], P(('groups', 'gx'), 'gy'), parts along dimension 0, may hold values from 0.5 to 2
- coriolis: float32 [3072], P('gy'), may hold values from 0.1 to 0.45
- land: int32 [256, 3072], P('gx', 'gy'), may hold values 0 or 1
- ice_tiles: int32 [4, 24], P('groups'), parts along dimension 0, may hold values 0 or 1
Outputs:
- velocity: float32 [2, 512, 3072], P(None, ('groups', 'gx'), 'gy'), parts along dimension 1
There are 2 independent parts, one for each index of `groups`. A program takes and returns all parts, laid end to end along the dimension named above; an argument that names none is the same for every part. Nothing has to cross between parts.
Inputs may be any that keep to these rules, and one draw needn't show every extreme that they name: 1 marks land. `ice_tiles`: 1 marks a tile with ice.
All inputs are finite; a program needn't handle non-finite values. No bound on the sum of `land` on one device may be relied on, other than what follows from the above.
Results may differ from a plain program's by a relative error of at most 0.00005.
Values sent between devices are 32-bit elements; how exact they have to be, the bound alone decides.
A program may use at most 64 MiB of HBM per device.

v0:
```python
import functools

import jax
import jax.numpy as jnp
from jax import lax
from jax.experimental import pallas as pl
from jax.experimental.pallas import tpu as pltpu
from jax.sharding import PartitionSpec as P

TILE = 128
LANES = 128
HALF = 64
HX = 8
COMP = 4
RELAX = 0.8
LAND_MASS = 4.0
MESH = pl.DeviceIdType.MESH
HIGH = lax.Precision.HIGHEST


def iota(shape, dim):
    return lax.broadcasted_iota(jnp.int32, shape, dim)


def dot(a, b):
    return jnp.dot(a, b, precision=HIGH, preferred_element_type=jnp.float32)


def shift(x, step, dim):
    size = x.shape[dim]
    return pltpu.roll(x, (-step) % size, dim)


def pair_sum(x, dim, step):
    odd = (iota(x.shape, dim) // step) % 2 == 1
    return x + jnp.where(odd, shift(x, -step, dim), shift(x, step, dim))


def odd_of_pair(x, dim, step):
    odd = (iota(x.shape, dim) // step) % 2 == 1
    return jnp.where(odd, x, shift(x, step, dim))


def coarsen(east, north, mass, rot, step):
    east = 0.25 * pair_sum(odd_of_pair(east, 0, step), 1, step)
    north = 0.25 * pair_sum(odd_of_pair(north, 1, step), 0, step)
    mass = 0.25 * pair_sum(pair_sum(mass, 0, step), 1, step)
    rot = 0.5 * pair_sum(rot, 1, step)
    return east, north, mass, rot


def stencil_of(east, north, mass, rot, keep, step):
    west = shift(east, -step, 0)
    south = shift(north, -step, 1)
    diag = mass + east + west + north + south
    return east, west, north, south, diag, keep * (RELAX / diag), rot


def off_diagonal(w, st, step):
    east, west, north, south, _, _, rot = st
    out = []
    for c in range(2):
        turned = -w[1] if c == 0 else w[0]
        out.append(
            east * shift(w[c], step, 0)
            + west * shift(w[c], -step, 0)
            + north * shift(w[c], step, 1)
            + south * shift(w[c], -step, 1)
            - rot * turned
        )
    return out


def from_zero(b, st):
    return [st[5] * b[c] for c in range(2)]


def residual_from_zero(b, w, st, step):
    off = off_diagonal(w, st, step)
    return [(1.0 - RELAX) * b[c] + off[c] for c in range(2)]


def sweep(w, b, st, step):
    off = off_diagonal(w, st, step)
    return [w[c] + st[5] * (b[c] - st[4] * w[c] + off[c]) for c in range(2)]


def restrict(r, step):
    return [0.25 * pair_sum(pair_sum(r[c], 0, step), 1, step) for c in range(2)]


def halo_place(k):
    return jnp.where(k < HALF, k // COMP, k // COMP + LANES - LANES // COMP)


def compact(x, own, select):
    block = COMP * LANES
    row, col = iota((block, LANES), 0), iota((block, LANES), 1)
    hit = (row == COMP * col + COMP - 1) if select else (row // COMP == col)
    m = jnp.where(hit, 1.0 / COMP, 0.0)
    row, col = iota((LANES, LANES), 0), iota((LANES, LANES), 1)
    hit = halo_place(row) == col
    if select:
        hit = hit & (row % COMP == COMP - 1)
    mh = jnp.where(hit, 1.0 / COMP, 0.0)
    parts = [
        dot(x[:, k * block : (k + 1) * block], m)
        for k in range(own // block)
    ]
    parts.append(dot(x[:, own:], mh))
    return jnp.concatenate(parts, 1)


def expand(x, own):
    block = COMP * LANES
    row, col = iota((LANES, block), 0), iota((LANES, block), 1)
    m = jnp.where(row == col // COMP, 1.0, 0.0)
    row, col = iota((LANES, LANES), 0), iota((LANES, LANES), 1)
    mh = jnp.where(row == halo_place(col), 1.0, 0.0)
    count = own // block
    parts = [
        dot(x[:, k * LANES : (k + 1) * LANES], m)
        for k in range(count)
    ]
    parts.append(dot(x[:, count * LANES :], mh))
    return jnp.concatenate(parts, 1)


def kernel(
    gx, gy, f_ref, v_ref, m_ref, cor_ref, land_ref, ice_ref, out_ref,
    ext, from_n, from_s, lev2, send, recv,
):
    nx, ny = v_ref.shape
    full = ny + LANES
    grp = lax.axis_index("groups")
    g = lax.axis_index("gx")
    r = lax.axis_index("gy")
    at_top = r == gy - 1
    at_bottom = r == 0
    right = (grp, lax.rem(g + 1, gx), r)
    left = (grp, lax.rem(g + gx - 1, gx), r)
    above = (grp, g, r + 1)
    below = (grp, g, r - 1)
    mirror = (grp, gx - 1 - g, r)

    barrier = pltpu.get_barrier_semaphore()

    def hello(device):
        pl.semaphore_signal(barrier, inc=1, device_id=device, device_id_type=MESH)

    hello(right)
    hello(left)

    @pl.when(at_top)
    def _():
        hello(mirror)

    @pl.when(jnp.logical_not(at_top))
    def _():
        hello(above)

    @pl.when(jnp.logical_not(at_bottom))
    def _():
        hello(below)

    land = land_ref[...].astype(jnp.float32)
    ocean = 1.0 - land
    tiles_x, tiles_y = ice_ref.shape
    ice_f = ice_ref[...].astype(jnp.float32)
    tile_row = (g * nx + iota((nx, tiles_y), 0)) // TILE
    ice_rows = jnp.zeros((nx, tiles_y), jnp.float32)
    for t in range(tiles_x):
        ice_rows = ice_rows + jnp.where(tile_row == t, ice_f[t : t + 1, :], 0.0)
    pick = jnp.where((r * ny + iota((tiles_y, ny), 1)) // TILE == iota((tiles_y, ny), 0), 1.0, 0.0)
    ice = jnp.dot(ice_rows, pick, preferred_element_type=jnp.float32)
    ext[0, 0:nx, 0:ny] = v_ref[...] * ice * ocean
    ext[1, 0:nx, 0:ny] = m_ref[...] * ocean + LAND_MASS * land
    ext[2, 0:nx, 0:ny] = f_ref[0] * ocean
    ext[3, 0:nx, 0:ny] = f_ref[1] * ocean
    ext[4, 0:nx, 0:ny] = jnp.broadcast_to(cor_ref[...], (nx, ny))

    pl.semaphore_wait(barrier, jnp.where(at_bottom, 3, 4))

    def copy(src, dst, k, device):
        return pltpu.make_async_remote_copy(
            src_ref=src, dst_ref=dst, send_sem=send.at[k], recv_sem=recv.at[k],
            device_id=device, device_id_type=MESH,
        )

    top_tile = ext.at[:, 0:nx, ny - LANES : ny]
    low_tile = ext.at[:, 0:nx, 0:LANES]
    to_mirror = copy(top_tile, from_n, 0, mirror)
    to_below = copy(low_tile, from_n, 2, below)
    to_above = copy(top_tile, from_s, 1, above)

    @pl.when(at_top)
    def _():
        to_mirror.start()

    @pl.when(jnp.logical_not(at_top))
    def _():
        to_above.start()

    @pl.when(jnp.logical_not(at_bottom))
    def _():
        to_below.start()

    def x_copy(buf, k, lo, hi, size, width, count):
        return (
            copy(buf.at[0:count, size - width : size, lo:hi],
                 buf.at[0:count, size + width : size + 2 * width, lo:hi], k, right),
            copy(buf.at[0:count, 0:width, lo:hi],
                 buf.at[0:count, size : size + width, lo:hi], k + 1, left),
        )

    bulk = x_copy(ext, 3, 0, ny, nx, HX, 4)
    for c in bulk:
        c.start()

    @pl.when(at_top)
    def _():
        to_mirror.wait()
        row, col = iota((LANES, LANES), 0), iota((LANES, LANES), 1)
        flip_l = jnp.where(row + col == LANES - 1, 1.0, 0.0)
        row, col = iota((nx, nx), 0), iota((nx, nx), 1)
        flip_r = jnp.where(row + col == nx - 1, 1.0, 0.0)
        for f in range(5):
            sign = -1.0 if f in (2, 3) else 1.0
            t = dot(from_n[f], flip_l)
            t = dot(sign * flip_r, t)
            ext[f, 0:nx, ny:full] = t

    @pl.when(jnp.logical_not(at_top))
    def _():
        to_above.wait_send()
        to_below.wait_recv()
        ext[:, 0:nx, ny:full] = from_n[...]

    south_part = iota((nx, LANES), 1) >= HALF

    @pl.when(at_bottom)
    def _():
        for f in range(5):
            if f == 0:
                fill = jnp.broadcast_to(ext[0, 0:nx, 0:1], (nx, LANES))
            else:
                fill = jnp.full((nx, LANES), 1.0 if f == 1 else 0.0, jnp.float32)
            ext[f, 0:nx, ny:full] = jnp.where(south_part, fill, ext[f, 0:nx, ny:full])

    @pl.when(jnp.logical_not(at_bottom))
    def _():
        to_below.wait_send()
        to_above.wait_recv()
        for f in range(5):
            ext[f, 0:nx, ny:full] = jnp.where(south_part, from_s[f], ext[f, 0:nx, ny:full])

    corner = x_copy(ext, 5, ny, full, nx, HX, 4)
    for c in corner:
        c.start()
    for c in bulk:
        c.wait()
    for c in corner:
        c.wait()

    visc, mass = ext[0], ext[1]
    src = [ext[2], ext[3]]
    rot = ext[4, 0:8]
    lane = iota((1, full), 1)
    keep = jnp.where((lane >= ny + HALF) & at_bottom, 0.0, 1.0)
    east = 0.5 * (visc + shift(visc, 1, 0))
    north = 0.5 * (visc + shift(visc, 1, 1))
    st0 = stencil_of(east, north, mass, rot[0:1], keep, 1)
    w0 = from_zero(src, st0)
    b1 = restrict(residual_from_zero(src, w0, st0, 1), 1)
    east1, north1, mass1, rot1 = coarsen(east, north, mass, rot, 1)
    st1 = stencil_of(east1, north1, mass1, rot1[0:1], keep, 2)
    w1 = from_zero(b1, st1)
    r1 = residual_from_zero(b1, w1, st1, 2)
    cx = nx // COMP
    row, col = iota((cx, nx), 0), iota((cx, nx), 1)
    mean_rows = jnp.where(col // COMP == row, 1.0 / COMP, 0.0)
    last_rows = jnp.where(col == COMP * row + COMP - 1, 1.0 / COMP, 0.0)
    avg = compact(jnp.concatenate([r1[0][0:nx], r1[1][0:nx], mass[0:nx], east[0:nx], rot], 0), ny, False)
    sel = compact(north[0:nx], ny, True)
    for k in range(4):
        lev2[k, 0:cx] = dot(last_rows if k == 3 else mean_rows, avg[k * nx : (k + 1) * nx])
    lev2[4, 0:cx] = dot(mean_rows, sel)
    rot2 = avg[4 * nx : 4 * nx + 8]
    third = x_copy(lev2, 7, 0, lev2.shape[2], cx, cx, 5)
    for c in third:
        c.start()
    for c in third:
        c.wait()
    b2 = [lev2[0], lev2[1]]
    mass2, east2, north2 = lev2[2], lev2[3], lev2[4]
    full2 = lev2.shape[2]
    lane2 = iota((1, full2), 1)
    used = (lane2 < ny // COMP + HALF // COMP) | (lane2 >= full2 - HALF // COMP)
    below2 = (lane2 >= full2 - HALF // COMP) & at_bottom
    keep2 = jnp.where(used & jnp.logical_not(below2), 1.0, 0.0)
    mass2 = jnp.where(used, mass2, 1.0)
    st2 = stencil_of(east2, north2, mass2, rot2[0:1], keep2, 1)
    w2 = from_zero(b2, st2)
    b3 = restrict(residual_from_zero(b2, w2, st2, 1), 1)
    east3, north3, mass3, rot3 = coarsen(east2, north2, mass2, rot2, 1)
    st3 = stencil_of(east3, north3, mass3, rot3[0:1], keep2, 2)
    e3 = from_zero(b3, st3)
    e3 = sweep(e3, b3, st3, 2)
    e3 = sweep(e3, b3, st3, 2)
    w2 = sweep([w2[c] + e3[c] for c in range(2)], b2, st2, 1)
    row, col = iota((nx + 2 * HX, 3 * cx), 0), iota((nx + 2 * HX, 3 * cx), 1)
    from_row = jnp.where(row < nx + HX, row // COMP, row // COMP + 3 * cx - (nx + 2 * HX) // COMP)
    spread = jnp.where(from_row == col, 1.0, 0.0)
    up = expand(jnp.concatenate([dot(spread, w2[c]) for c in range(2)], 0), ny)
    up = [up[0 : nx + 2 * HX], up[nx + 2 * HX :]]
    e1 = sweep([w1[c] + up[c] for c in range(2)], b1, st1, 2)
    w0 = sweep([w0[c] + e1[c] for c in range(2)], src, st0, 1)
    for c in range(2):
        out_ref[c] = w0[c][0:nx, 0:ny]


def local(gx, gy, forcing, viscosity, mass, coriolis, land, ice_tiles):
    nx, ny = viscosity.shape
    ext = (nx + 2 * HX, ny + LANES)
    return pl.pallas_call(
        functools.partial(kernel, gx, gy),
        out_shape=jax.ShapeDtypeStruct(forcing.shape, jnp.float32),
        in_specs=[pl.BlockSpec(memory_space=pltpu.VMEM)] * 6,
        out_specs=pl.BlockSpec(memory_space=pltpu.VMEM),
        scratch_shapes=[
            pltpu.VMEM((5,) + ext, jnp.float32),
            pltpu.VMEM((5, nx, LANES), jnp.float32),
            pltpu.VMEM((5, nx, LANES), jnp.float32),
            pltpu.VMEM((5, 3 * (nx // COMP), ny // COMP + LANES), jnp.float32),
            pltpu.SemaphoreType.DMA((9,)),
            pltpu.SemaphoreType.DMA((9,)),
        ],
        compiler_params=pltpu.CompilerParams(collective_id=0, has_side_effects=True),
    )(forcing, viscosity, mass, coriolis.reshape(1, -1), land, ice_tiles)


def solution(mesh):
    return jax.shard_map(
        functools.partial(local, mesh.shape["gx"], mesh.shape["gy"]),
        mesh=mesh,
        in_specs=(
            P(None, ("groups", "gx"), "gy"),
            P(("groups", "gx"), "gy"),
            P(("groups", "gx"), "gy"),
            P("gy"),
            P("gx", "gy"),
            P("groups", None),
        ),
        out_specs=P(None, ("groups", "gx"), "gy"),
        check_vma=False,
    )
```

profile of v0, /device:TPU:0, one launch (start us, length us, event | category | flops | bytes accessed | tf_op | source)
XLA Modules:
  0.0 32.5 jit_solution(5515728740937895709)
XLA Ops:
  0.0 1.3 %reshape.3.cor_ref = f32[1,1536]{1,0:T(1,128)} reshape(f32[1536]{0:T(1024)} %param.9) | data formatting | bytes 12288 | tf_op jit(solution)/shard_map/reshape | solution.py:339
  1.3 29.4 %shard_map.64 = f32[2,32,1536]{2,1,0:T(8,128)} custom-call(f32[2,32,1536]{2,1,0:T(8,128)} %f_ref.1, f32[32,1536]{1,0:T(8,128)} %v_ref.1, f32[32,1536]{1,0:T(8,128)} %m_ref.1, f32[1,1536]{1,0:T(1,128)} %reshape.3.cor_ref, s32[32,1536]{1,0:T(8,128)} %land_ref.1, s32[2,24]{1,0:T(2,128)} %ice_ref.1), custom_call_target="tpu_custom_call" | custom-call | tf_op jit(solution)/shard_map/pallas_call | solution.py:325
  30.7 1.8 %copy.8 = f32[2,32,1536]{2,1,0:T(8,128)} copy(f32[2,32,1536]{2,1,0:T(8,128)} %shard_map.64) | data formatting | bytes 786432
where the time goes:
time: 32.7 us; the launch traced here: 32.5 us
  Pallas kernels  29.4 us (90%)
  local copies, waits for them, and re-layouts  3.06 us (9%)
    pallas_call x1, Pallas kernels, local(): pl.pallas_call(functools.partial(kernel, gx, gy), out_shape=jax.ShapeDtyp...  29.4 us
    unnamed x1, local copies, waits for them, and re-layouts  1.77 us
    reshape x1, local copies, waits for them, and re-layouts, local(): coriolis.reshape(1, -1)  1.29 us

commit v1 on v0

--- a/solution.py
+++ b/solution.py
@@ -9,7 +9,7 @@
 
 TILE = 128
 LANES = 128
-HALF = 64
+HALF = 32
 HX = 8
 COMP = 4
 RELAX = 0.8
@@ -126,9 +126,22 @@
     return jnp.concatenate(parts, 1)
 
 
+DEPTH = (6, 5, 5, 5)
+FILL = (0.0, 1.0, 0.0, 0.0)
+
+
+def edges():
+    offset, out = 0, []
+    for depth in DEPTH:
+        out.append((offset, depth))
+        offset += depth
+    return out
+
+
 def kernel(
-    gx, gy, f_ref, v_ref, m_ref, cor_ref, land_ref, ice_ref, out_ref,
-    ext, from_n, from_s, lev2, send, recv,
+    gx, gy, f_hbm, v_hbm, m_hbm, cor_ref, land_hbm, ice_ref, out_ref,
+    f_ref, v_ref, m_ref, land_ref, ext, rotx, low_pack, top_pack, from_n, from_s,
+    to_r, to_l, from_r, from_l, lev2, load, send, recv,
 ):
     nx, ny = v_ref.shape
     full = ny + LANES
@@ -137,6 +150,8 @@
     r = lax.axis_index("gy")
     at_top = r == gy - 1
     at_bottom = r == 0
+    not_top = jnp.logical_not(at_top)
+    not_bottom = jnp.logical_not(at_bottom)
     right = (grp, lax.rem(g + 1, gx), r)
     left = (grp, lax.rem(g + gx - 1, gx), r)
     above = (grp, g, r + 1)
@@ -148,23 +163,27 @@
     def hello(device):
         pl.semaphore_signal(barrier, inc=1, device_id=device, device_id_type=MESH)
 
+    @pl.when(at_top)
+    def _():
+        hello(mirror)
+
     hello(right)
     hello(left)
 
-    @pl.when(at_top)
-    def _():
-        hello(mirror)
-
-    @pl.when(jnp.logical_not(at_top))
+    @pl.when(not_top)
     def _():
         hello(above)
 
-    @pl.when(jnp.logical_not(at_bottom))
+    @pl.when(not_bottom)
     def _():
         hello(below)
 
-    land = land_ref[...].astype(jnp.float32)
-    ocean = 1.0 - land
+    loads = [
+        pltpu.make_async_copy(a, b, load.at[k])
+        for k, (a, b) in enumerate(((land_hbm, land_ref), (v_hbm, v_ref), (m_hbm, m_ref), (f_hbm, f_ref)))
+    ]
+    for c in loads:
+        c.start()
     tiles_x, tiles_y = ice_ref.shape
     ice_f = ice_ref[...].astype(jnp.float32)
     tile_row = (g * nx + iota((nx, tiles_y), 0)) // TILE
@@ -173,11 +192,32 @@
         ice_rows = ice_rows + jnp.where(tile_row == t, ice_f[t : t + 1, :], 0.0)
     pick = jnp.where((r * ny + iota((tiles_y, ny), 1)) // TILE == iota((tiles_y, ny), 0), 1.0, 0.0)
     ice = jnp.dot(ice_rows, pick, preferred_element_type=jnp.float32)
+    rotx[:, 0:ny] = jnp.broadcast_to(cor_ref[...].reshape(1, ny), (8, ny))
+    for f in range(4):
+        ext[f, nx:, :] = jnp.full((2 * HX, full), FILL[f], jnp.float32)
+    for c in loads:
+        c.wait()
+    land = land_ref[...].astype(jnp.float32)
+    ocean = 1.0 - land
     ext[0, 0:nx, 0:ny] = v_ref[...] * ice * ocean
     ext[1, 0:nx, 0:ny] = m_ref[...] * ocean + LAND_MASS * land
     ext[2, 0:nx, 0:ny] = f_ref[0] * ocean
     ext[3, 0:nx, 0:ny] = f_ref[1] * ocean
-    ext[4, 0:nx, 0:ny] = jnp.broadcast_to(cor_ref[...], (nx, ny))
+
+    group = iota((nx, LANES), 1) // HALF
+    low, top = jnp.zeros((nx, LANES), jnp.float32), jnp.zeros((nx, LANES), jnp.float32)
+    for f in range(4):
+        low = jnp.where(group == f, pltpu.roll(ext[f, 0:nx, 0:LANES], HALF * f, 1), low)
+        top = jnp.where(
+            group == f, pltpu.roll(ext[f, 0:nx, ny - LANES : ny], (HALF * (f + 1)) % LANES, 1), top)
+    low_pack[0:nx] = low
+    low_pack[nx:] = rotx[:, 0:LANES]
+    top_pack[0:nx] = top
+    top_pack[nx:] = pltpu.roll(rotx[:, ny - LANES : ny], HALF, 1)
+
+    for f, (o, d) in enumerate(edges()):
+        to_r[o : o + d, 0:ny] = ext[f, nx - d : nx, 0:ny]
+        to_l[o : o + d, 0:ny] = ext[f, 0:d, 0:ny]
 
     pl.semaphore_wait(barrier, jnp.where(at_bottom, 3, 4))
 
@@ -187,33 +227,29 @@
             device_id=device, device_id_type=MESH,
         )
 
-    top_tile = ext.at[:, 0:nx, ny - LANES : ny]
-    low_tile = ext.at[:, 0:nx, 0:LANES]
-    to_mirror = copy(top_tile, from_n, 0, mirror)
-    to_below = copy(low_tile, from_n, 2, below)
-    to_above = copy(top_tile, from_s, 1, above)
+    to_mirror = copy(top_pack, from_n, 0, mirror)
+    to_above = copy(top_pack, from_s, 1, above)
+    to_below = copy(low_pack, from_n, 2, below)
 
     @pl.when(at_top)
     def _():
         to_mirror.start()
 
-    @pl.when(jnp.logical_not(at_top))
+    @pl.when(not_top)
     def _():
         to_above.start()
 
-    @pl.when(jnp.logical_not(at_bottom))
+    @pl.when(not_bottom)
     def _():
         to_below.start()
 
-    def x_copy(buf, k, lo, hi, size, width, count):
+    def strips(k, lo, hi):
         return (
-            copy(buf.at[0:count, size - width : size, lo:hi],
-                 buf.at[0:count, size + width : size + 2 * width, lo:hi], k, right),
-            copy(buf.at[0:count, 0:width, lo:hi],
-                 buf.at[0:count, size : size + width, lo:hi], k + 1, left),
+            copy(to_r.at[:, lo:hi], from_l.at[:, lo:hi], k, right),
+            copy(to_l.at[:, lo:hi], from_r.at[:, lo:hi], k + 1, left),
         )
 
-    bulk = x_copy(ext, 3, 0, ny, nx, HX, 4)
+    bulk = strips(3, 0, ny)
     for c in bulk:
         c.start()
 
@@ -221,54 +257,77 @@
     def _():
         to_mirror.wait()
         row, col = iota((LANES, LANES), 0), iota((LANES, LANES), 1)
-        flip_l = jnp.where(row + col == LANES - 1, 1.0, 0.0)
+        flip_l = jnp.where((row // HALF == col // HALF) & (row % HALF + col % HALF == HALF - 1), 1.0, 0.0)
         row, col = iota((nx, nx), 0), iota((nx, nx), 1)
         flip_r = jnp.where(row + col == nx - 1, 1.0, 0.0)
-        for f in range(5):
-            sign = -1.0 if f in (2, 3) else 1.0
-            t = dot(from_n[f], flip_l)
-            t = dot(sign * flip_r, t)
-            ext[f, 0:nx, ny:full] = t
-
-    @pl.when(jnp.logical_not(at_top))
+        t = dot(from_n[...], flip_l)
+        from_n[0:nx] = dot(flip_r, t[0:nx]) * jnp.where(group >= 2, -1.0, 1.0)
+        from_n[nx:] = t[nx:]
+
+    @pl.when(not_top)
     def _():
         to_above.wait_send()
         to_below.wait_recv()
-        ext[:, 0:nx, ny:full] = from_n[...]
-
-    south_part = iota((nx, LANES), 1) >= HALF
-
-    @pl.when(at_bottom)
-    def _():
-        for f in range(5):
-            if f == 0:
-                fill = jnp.broadcast_to(ext[0, 0:nx, 0:1], (nx, LANES))
-            else:
-                fill = jnp.full((nx, LANES), 1.0 if f == 1 else 0.0, jnp.float32)
-            ext[f, 0:nx, ny:full] = jnp.where(south_part, fill, ext[f, 0:nx, ny:full])
-
-    @pl.when(jnp.logical_not(at_bottom))
+
+    @pl.when(not_bottom)
     def _():
         to_below.wait_send()
         to_above.wait_recv()
-        for f in range(5):
-            ext[f, 0:nx, ny:full] = jnp.where(south_part, from_s[f], ext[f, 0:nx, ny:full])
-
-    corner = x_copy(ext, 5, ny, full, nx, HX, 4)
+
+    @pl.when(at_bottom)
+    def _():
+        from_s[...] = jnp.zeros(from_s.shape, jnp.float32)
+        from_s[0:nx] = jnp.where(
+            group == 0, jnp.broadcast_to(ext[0, 0:nx, 0:1], (nx, LANES)), jnp.where(group == 1, 1.0, 0.0))
+
+    for f in range(4):
+        n = pltpu.roll(from_n[0:nx], (LANES - HALF * f) % LANES, 1)
+        s = pltpu.roll(from_s[0:nx], (LANES - HALF * (f + 1)) % LANES, 1)
+        ext[f, 0:nx, ny:full] = jnp.where(group == 0, n, jnp.where(group == LANES // HALF - 1, s, FILL[f]))
+    group8 = iota((8, LANES), 1) // HALF
+    rotx[:, ny:full] = jnp.where(group8 == 0, from_n[nx:], pltpu.roll(from_s[nx:], LANES - HALF, 1))
+    for f, (o, d) in enumerate(edges()):
+        to_r[o : o + d, ny:full] = ext[f, nx - d : nx, ny:full]
+        to_l[o : o + d, ny:full] = ext[f, 0:d, ny:full]
+
+    corner = strips(5, ny, full)
     for c in corner:
         c.start()
     for c in bulk:
         c.wait()
     for c in corner:
         c.wait()
+    for f, (o, d) in enumerate(edges()):
+        ext[f, nx : nx + d] = from_r[o : o + d]
+        ext[f, nx + 2 * HX - d : nx + 2 * HX] = from_l[o : o + d]
 
     visc, mass = ext[0], ext[1]
     src = [ext[2], ext[3]]
-    rot = ext[4, 0:8]
+    rot = rotx[...]
     lane = iota((1, full), 1)
-    keep = jnp.where((lane >= ny + HALF) & at_bottom, 0.0, 1.0)
+    used = (lane < ny + HALF) | ((lane >= full - HALF) & not_bottom)
+    keep = jnp.where(used, 1.0, 0.0)
     east = 0.5 * (visc + shift(visc, 1, 0))
     north = 0.5 * (visc + shift(visc, 1, 1))
+    cx = nx // COMP
+    row, col = iota((cx, nx), 0), iota((cx, nx), 1)
+    mean_rows = jnp.where(col // COMP == row, 1.0 / COMP, 0.0)
+    last_rows = jnp.where(col == COMP * row + COMP - 1, 1.0 / COMP, 0.0)
+    avg = compact(jnp.concatenate([mass[0:nx], east[0:nx], rot], 0), ny, False)
+    lev2[2, 0:cx] = dot(mean_rows, avg[0:nx])
+    lev2[3, 0:cx] = dot(last_rows, avg[nx : 2 * nx])
+    lev2[4, 0:cx] = dot(mean_rows, compact(north[0:nx], ny, True))
+    rot2 = avg[2 * nx : 2 * nx + 8]
+
+    def blocks(k, lo, hi):
+        return (
+            copy(lev2.at[lo:hi, 0:cx], lev2.at[lo:hi, 2 * cx : 3 * cx], k, right),
+            copy(lev2.at[lo:hi, 0:cx], lev2.at[lo:hi, cx : 2 * cx], k + 1, left),
+        )
+
+    first = blocks(7, 2, 5)
+    for c in first:
+        c.start()
     st0 = stencil_of(east, north, mass, rot[0:1], keep, 1)
     w0 = from_zero(src, st0)
     b1 = restrict(residual_from_zero(src, w0, st0, 1), 1)
@@ -276,20 +335,15 @@
     st1 = stencil_of(east1, north1, mass1, rot1[0:1], keep, 2)
     w1 = from_zero(b1, st1)
     r1 = residual_from_zero(b1, w1, st1, 2)
-    cx = nx // COMP
-    row, col = iota((cx, nx), 0), iota((cx, nx), 1)
-    mean_rows = jnp.where(col // COMP == row, 1.0 / COMP, 0.0)
-    last_rows = jnp.where(col == COMP * row + COMP - 1, 1.0 / COMP, 0.0)
-    avg = compact(jnp.concatenate([r1[0][0:nx], r1[1][0:nx], mass[0:nx], east[0:nx], rot], 0), ny, False)
-    sel = compact(north[0:nx], ny, True)
-    for k in range(4):
-        lev2[k, 0:cx] = dot(last_rows if k == 3 else mean_rows, avg[k * nx : (k + 1) * nx])
-    lev2[4, 0:cx] = dot(mean_rows, sel)
-    rot2 = avg[4 * nx : 4 * nx + 8]
-    third = x_copy(lev2, 7, 0, lev2.shape[2], cx, cx, 5)
-    for c in third:
+    avg = compact(jnp.concatenate([r1[0][0:nx], r1[1][0:nx]], 0), ny, False)
+    for k in range(2):
+        lev2[k, 0:cx] = dot(mean_rows, avg[k * nx : (k + 1) * nx])
+    second = blocks(9, 0, 2)
+    for c in second:
         c.start()
-    for c in third:
+    for c in first:
+        c.wait()
+    for c in second:
         c.wait()
     b2 = [lev2[0], lev2[1]]
     mass2, east2, north2 = lev2[2], lev2[3], lev2[4]
@@ -322,21 +376,32 @@
 def local(gx, gy, forcing, viscosity, mass, coriolis, land, ice_tiles):
     nx, ny = viscosity.shape
     ext = (nx + 2 * HX, ny + LANES)
+    strip = pltpu.VMEM((nx + 8, LANES), jnp.float32)
+    height = -(-sum(DEPTH) // 8) * 8
+    side = pltpu.VMEM((height, ny + LANES), jnp.float32)
+    anyspace = pl.BlockSpec(memory_space=pl.ANY)
+    vmem = pl.BlockSpec(memory_space=pltpu.VMEM)
     return pl.pallas_call(
         functools.partial(kernel, gx, gy),
         out_shape=jax.ShapeDtypeStruct(forcing.shape, jnp.float32),
-        in_specs=[pl.BlockSpec(memory_space=pltpu.VMEM)] * 6,
-        out_specs=pl.BlockSpec(memory_space=pltpu.VMEM),
+        in_specs=[anyspace, anyspace, anyspace, vmem, anyspace, vmem],
+        out_specs=vmem,
         scratch_shapes=[
-            pltpu.VMEM((5,) + ext, jnp.float32),
-            pltpu.VMEM((5, nx, LANES), jnp.float32),
-            pltpu.VMEM((5, nx, LANES), jnp.float32),
+            pltpu.VMEM(forcing.shape, jnp.float32),
+            pltpu.VMEM((nx, ny), jnp.float32),
+            pltpu.VMEM((nx, ny), jnp.float32),
+            pltpu.VMEM((nx, ny), jnp.int32),
+            pltpu.VMEM((4,) + ext, jnp.float32),
+            pltpu.VMEM((8, ny + LANES), jnp.float32),
+            strip, strip, strip, strip,
+            side, side, side, side,
             pltpu.VMEM((5, 3 * (nx // COMP), ny // COMP + LANES), jnp.float32),
-            pltpu.SemaphoreType.DMA((9,)),
-            pltpu.SemaphoreType.DMA((9,)),
+            pltpu.SemaphoreType.DMA((4,)),
+            pltpu.SemaphoreType.DMA((11,)),
+            pltpu.SemaphoreType.DMA((11,)),
         ],
         compiler_params=pltpu.CompilerParams(collective_id=0, has_side_effects=True),
-    )(forcing, viscosity, mass, coriolis.reshape(1, -1), land, ice_tiles)
+    )(forcing, viscosity, mass, coriolis, land, ice_tiles)
 
 
 def solution(mesh):

time: 32.7 us -> 28 us (0.86)
  Pallas kernels: 29.4 us -> 26 us
  local copies, waits for them, and re-layouts: 3.06 us -> 1.77 us
    pallas_call x1, Pallas kernels: 29.4 us -> 26 us  [local(): pl.pallas_call(functools.partial(kernel, gx, gy), out_shape=jax.ShapeDtyp...]
    reshape x1 -> x0, local copies, waits for them, and re-layouts: 1.29 us -> none  [local(): coriolis.reshape(1, -1)]
where the time goes in v1:
time: 28 us; the launch traced here: 27.7 us
  Pallas kernels  26 us (93%)
  local copies, waits for them, and re-layouts  1.77 us (6%)
    pallas_call x1, Pallas kernels, local(): pl.pallas_call(functools.partial(kernel, gx, gy), out_shape=jax.ShapeDtyp...  26 us
    unnamed x1, local copies, waits for them, and re-layouts  1.77 us

profile of v1, /device:TPU:0, one launch (start us, length us, event | category | flops | bytes accessed | tf_op | source)
XLA Modules:
  0.0 27.7 jit_solution(13581226374468996240)
XLA Ops:
  0.0 26.0 %shard_map.64 = f32[2,32,1536]{2,1,0:T(8,128)} custom-call(f32[2,32,1536]{2,1,0:T(8,128)} %f_hbm.1, f32[32,1536]{1,0:T(8,128)} %v_hbm.1, f32[32,1536]{1,0:T(8,128)} %m_hbm.1, f32[1536]{0:T(1024)} %cor_ref.1, s32[32,1536]{1,0:T(8,128)} %land_hbm.1, s32[2,24]{1,0:T(2,128)} %ice_ref.1), custom_call_target="tpu_custom_call" | custom-call | tf_op jit(solution)/shard_map/pallas_call | solution.py:384
  26.0 1.8 %copy.8 = f32[2,32,1536]{2,1,0:T(8,128)} copy(f32[2,32,1536]{2,1,0:T(8,128)} %shard_map.64) | data formatting | bytes 786432

commit v2 on v1

--- a/solution.py
+++ b/solution.py
@@ -15,15 +15,28 @@
 RELAX = 0.8
 LAND_MASS = 4.0
 MESH = pl.DeviceIdType.MESH
-HIGH = lax.Precision.HIGHEST
 
 
 def iota(shape, dim):
     return lax.broadcasted_iota(jnp.int32, shape, dim)
 
 
-def dot(a, b):
-    return jnp.dot(a, b, precision=HIGH, preferred_element_type=jnp.float32)
+def parts(x):
+    high = x.astype(jnp.bfloat16)
+    rest = x - high.astype(jnp.float32)
+    middle = rest.astype(jnp.bfloat16)
+    low = (rest - middle.astype(jnp.float32)).astype(jnp.bfloat16)
+    return high, middle, low
+
+
+def pick_right(x, m):
+    m = m.astype(jnp.bfloat16)
+    return sum(jnp.dot(p, m, preferred_element_type=jnp.float32) for p in parts(x))
+
+
+def pick_left(m, x):
+    m = m.astype(jnp.bfloat16)
+    return sum(jnp.dot(m, p, preferred_element_type=jnp.float32) for p in parts(x))
 
 
 def shift(x, step, dim):
@@ -103,12 +116,12 @@
     if select:
         hit = hit & (row % COMP == COMP - 1)
     mh = jnp.where(hit, 1.0 / COMP, 0.0)
-    parts = [
-        dot(x[:, k * block : (k + 1) * block], m)
+    out = [
+        pick_right(x[:, k * block : (k + 1) * block], m)
         for k in range(own // block)
     ]
-    parts.append(dot(x[:, own:], mh))
-    return jnp.concatenate(parts, 1)
+    out.append(pick_right(x[:, own:], mh))
+    return jnp.concatenate(out, 1)
 
 
 def expand(x, own):
@@ -118,12 +131,12 @@
     row, col = iota((LANES, LANES), 0), iota((LANES, LANES), 1)
     mh = jnp.where(row == halo_place(col), 1.0, 0.0)
     count = own // block
-    parts = [
-        dot(x[:, k * LANES : (k + 1) * LANES], m)
+    out = [
+        pick_right(x[:, k * LANES : (k + 1) * LANES], m)
         for k in range(count)
     ]
-    parts.append(dot(x[:, count * LANES :], mh))
-    return jnp.concatenate(parts, 1)
+    out.append(pick_right(x[:, count * LANES :], mh))
+    return jnp.concatenate(out, 1)
 
 
 DEPTH = (6, 5, 5, 5)
@@ -260,8 +273,8 @@
         flip_l = jnp.where((row // HALF == col // HALF) & (row % HALF + col % HALF == HALF - 1), 1.0, 0.0)
         row, col = iota((nx, nx), 0), iota((nx, nx), 1)
         flip_r = jnp.where(row + col == nx - 1, 1.0, 0.0)
-        t = dot(from_n[...], flip_l)
-        from_n[0:nx] = dot(flip_r, t[0:nx]) * jnp.where(group >= 2, -1.0, 1.0)
+        t = pick_right(from_n[...], flip_l)
+        from_n[0:nx] = pick_left(flip_r, t[0:nx]) * jnp.where(group >= 2, -1.0, 1.0)
         from_n[nx:] = t[nx:]
 
     @pl.when(not_top)
@@ -293,41 +306,47 @@
     corner = strips(5, ny, full)
     for c in corner:
         c.start()
+    own_v, own_m, rot = ext[0, 0:nx], ext[1, 0:nx], rotx[...]
+    own_e = 0.5 * (own_v + shift(own_v, 1, 0))
+    own_n = 0.5 * (own_v + shift(own_v, 1, 1))
+    cx = nx // COMP
+    row, col = iota((cx, nx), 0), iota((cx, nx), 1)
+    mean_rows = jnp.where(col // COMP == row, 1.0 / COMP, 0.0)
+    last_rows = jnp.where(col == COMP * row + COMP - 1, 1.0 / COMP, 0.0)
+    avg = compact(jnp.concatenate([own_m, own_e, rot], 0), ny, False)
+    lev2[2, 0:cx] = pick_left(mean_rows, avg[0:nx])
+    lev2[3, 0:cx] = pick_left(last_rows, avg[nx : 2 * nx])
+    lev2[4, 0:cx] = pick_left(mean_rows, compact(own_n, ny, True))
+    rot2 = avg[2 * nx : 2 * nx + 8]
+
+    def blocks(k, lo, hi):
+        return (
+            copy(lev2.at[lo:hi, 0:cx], lev2.at[lo:hi, 2 * cx : 3 * cx], k, right),
+            copy(lev2.at[lo:hi, 0:cx], lev2.at[lo:hi, cx : 2 * cx], k + 1, left),
+        )
+
+    first = blocks(7, 2, 5)
     for c in bulk:
         c.wait()
     for c in corner:
         c.wait()
+    for c in first:
+        c.start()
     for f, (o, d) in enumerate(edges()):
         ext[f, nx : nx + d] = from_r[o : o + d]
         ext[f, nx + 2 * HX - d : nx + 2 * HX] = from_l[o : o + d]
 
     visc, mass = ext[0], ext[1]
     src = [ext[2], ext[3]]
-    rot = rotx[...]
     lane = iota((1, full), 1)
     used = (lane < ny + HALF) | ((lane >= full - HALF) & not_bottom)
     keep = jnp.where(used, 1.0, 0.0)
     east = 0.5 * (visc + shift(visc, 1, 0))
     north = 0.5 * (visc + shift(visc, 1, 1))
-    cx = nx // COMP
-    row, col = iota((cx, nx), 0), iota((cx, nx), 1)
-    mean_rows = jnp.where(col // COMP == row, 1.0 / COMP, 0.0)
-    last_rows = jnp.where(col == COMP * row + COMP - 1, 1.0 / COMP, 0.0)
-    avg = compact(jnp.concatenate([mass[0:nx], east[0:nx], rot], 0), ny, False)
-    lev2[2, 0:cx] = dot(mean_rows, avg[0:nx])
-    lev2[3, 0:cx] = dot(last_rows, avg[nx : 2 * nx])
-    lev2[4, 0:cx] = dot(mean_rows, compact(north[0:nx], ny, True))
-    rot2 = avg[2 * nx : 2 * nx + 8]
-
-    def blocks(k, lo, hi):
-        return (
-            copy(lev2.at[lo:hi, 0:cx], lev2.at[lo:hi, 2 * cx : 3 * cx], k, right),
-            copy(lev2.at[lo:hi, 0:cx], lev2.at[lo:hi, cx : 2 * cx], k + 1, left),
-        )
-
-    first = blocks(7, 2, 5)
-    for c in first:
-        c.start()
+    face = compact(
+        jnp.concatenate([0.5 * (visc[nx - 1 : nx] + visc[nx : nx + 1]),
+                         0.5 * (visc[nx + 2 * HX - 1 : nx + 2 * HX] + visc[0:1])] * 4, 0), ny, False)
+    face = (1.0 / COMP) * face
     st0 = stencil_of(east, north, mass, rot[0:1], keep, 1)
     w0 = from_zero(src, st0)
     b1 = restrict(residual_from_zero(src, w0, st0, 1), 1)
@@ -337,16 +356,15 @@
     r1 = residual_from_zero(b1, w1, st1, 2)
     avg = compact(jnp.concatenate([r1[0][0:nx], r1[1][0:nx]], 0), ny, False)
     for k in range(2):
-        lev2[k, 0:cx] = dot(mean_rows, avg[k * nx : (k + 1) * nx])
+        lev2[k, 0:cx] = pick_left(mean_rows, avg[k * nx : (k + 1) * nx])
     second = blocks(9, 0, 2)
     for c in second:
         c.start()
     for c in first:
         c.wait()
-    for c in second:
-        c.wait()
-    b2 = [lev2[0], lev2[1]]
     mass2, east2, north2 = lev2[2], lev2[3], lev2[4]
+    row2 = iota(east2.shape, 0)
+    east2 = jnp.where(row2 == cx - 1, face[0:1], jnp.where(row2 == 3 * cx - 1, face[1:2], east2))
     full2 = lev2.shape[2]
     lane2 = iota((1, full2), 1)
     used = (lane2 < ny // COMP + HALF // COMP) | (lane2 >= full2 - HALF // COMP)
@@ -354,10 +372,13 @@
     keep2 = jnp.where(used & jnp.logical_not(below2), 1.0, 0.0)
     mass2 = jnp.where(used, mass2, 1.0)
     st2 = stencil_of(east2, north2, mass2, rot2[0:1], keep2, 1)
+    east3, north3, mass3, rot3 = coarsen(east2, north2, mass2, rot2, 1)
+    st3 = stencil_of(east3, north3, mass3, rot3[0:1], keep2, 2)
+    for c in second:
+        c.wait()
+    b2 = [lev2[0], lev2[1]]
     w2 = from_zero(b2, st2)
     b3 = restrict(residual_from_zero(b2, w2, st2, 1), 1)
-    east3, north3, mass3, rot3 = coarsen(east2, north2, mass2, rot2, 1)
-    st3 = stencil_of(east3, north3, mass3, rot3[0:1], keep2, 2)
     e3 = from_zero(b3, st3)
     e3 = sweep(e3, b3, st3, 2)
     e3 = sweep(e3, b3, st3, 2)
@@ -365,12 +386,19 @@
     row, col = iota((nx + 2 * HX, 3 * cx), 0), iota((nx + 2 * HX, 3 * cx), 1)
     from_row = jnp.where(row < nx + HX, row // COMP, row // COMP + 3 * cx - (nx + 2 * HX) // COMP)
     spread = jnp.where(from_row == col, 1.0, 0.0)
-    up = expand(jnp.concatenate([dot(spread, w2[c]) for c in range(2)], 0), ny)
+    up = expand(jnp.concatenate([pick_left(spread, w2[c]) for c in range(2)], 0), ny)
     up = [up[0 : nx + 2 * HX], up[nx + 2 * HX :]]
     e1 = sweep([w1[c] + up[c] for c in range(2)], b1, st1, 2)
-    w0 = sweep([w0[c] + e1[c] for c in range(2)], src, st0, 1)
+    def crop(x):
+        return x[0:nx, 0:ny]
+
+    w0 = [w0[c] + e1[c] for c in range(2)]
+    east, west, north, south, diag, inverse = [crop(x) for x in st0[:6]]
     for c in range(2):
-        out_ref[c] = w0[c][0:nx, 0:ny]
+        w, turned = w0[c], crop(-w0[1] if c == 0 else w0[0])
+        out_ref[c] = crop(w) + inverse * (
+            crop(src[c]) - diag * crop(w) + east * crop(shift(w, 1, 0)) + west * crop(shift(w, -1, 0))
+            + north * crop(shift(w, 1, 1)) + south * crop(shift(w, -1, 1)) - rot[0:1, 0:ny] * turned)
 
 
 def local(gx, gy, forcing, viscosity, mass, coriolis, land, ice_tiles):

time: 28 us -> 26 us (0.929)
  Pallas kernels: 26 us -> 24 us
    pallas_call x1, Pallas kernels: 26 us -> 24 us  [local(): pl.pallas_call(functools.partial(kernel, gx, gy), out_shape=jax.ShapeDtyp...]
where the time goes in v2:
time: 26 us; the launch traced here: 25.8 us
  Pallas kernels  24 us (92%)
  local copies, waits for them, and re-layouts  1.77 us (7%)
    pallas_call x1, Pallas kernels, local(): pl.pallas_call(functools.partial(kernel, gx, gy), out_shape=jax.ShapeDtyp...  24 us
    unnamed x1, local copies, waits for them, and re-layouts  1.77 us

profile of v2, /device:TPU:0, one launch (start us, length us, event | category | flops | bytes accessed | tf_op | source)
XLA Modules:
  0.0 25.8 jit_solution(7992219784234259408)
XLA Ops:
  0.0 24.0 %shard_map.64 = f32[2,32,1536]{2,1,0:T(8,128)} custom-call(f32[2,32,1536]{2,1,0:T(8,128)} %f_hbm.1, f32[32,1536]{1,0:T(8,128)} %v_hbm.1, f32[32,1536]{1,0:T(8,128)} %m_hbm.1, f32[1536]{0:T(1024)} %cor_ref.1, s32[32,1536]{1,0:T(8,128)} %land_hbm.1, s32[2,24]{1,0:T(2,128)} %ice_ref.1), custom_call_target="tpu_custom_call" | custom-call | tf_op jit(solution)/shard_map/pallas_call | solution.py:412
  24.0 1.8 %copy.8 = f32[2,32,1536]{2,1,0:T(8,128)} copy(f32[2,32,1536]{2,1,0:T(8,128)} %shard_map.64) | data formatting | bytes 786432
